TPU v7x, 32 devices: a whole 2x2x4 slice. The times are simulated.
32 devices in a mesh: groups: 2 (over y), cols: 4 (over z), rows: 4 (over x, core).
Axes of the slice: x: 2, y: 2, z: 4, core: 2. Of those that a mesh axis runs over, the one named last changes fastest.
Arguments:
- base_field: float32 [320, 64, 512], P(None, ('groups', 'cols'), 'rows'), parts along dimension 1, may hold values from -6 to 6
- control_field: float32 [320, 64, 512], P(None, ('groups', 'cols', 'rows')), parts along dimension 1, may hold values from -6 to 6
- first_kernel: bfloat16 [9, 320, 320], replicated, may hold values from -0.109375 to 0.109375
- second_kernel: bfloat16 [9, 320, 320], replicated, may hold values from -0.109375 to 0.109375
- control_kernel: bfloat16 [9, 320, 320], replicated, may hold values from -0.109375 to 0.109375
- first_bias: float32 [320], replicated, may hold values from -3 to 3
- second_bias: float32 [320], replicated, may hold values from -3 to 3
- control_bias: float32 [320], replicated, may hold values from -3 to 3
- to_control: bfloat16 [320, 320], replicated, may hold values from -0.3125 to 0.3125
- to_base: bfloat16 [320, 320], replicated, may hold values from -0.3125 to 0.3125
Outputs:
- base_out: float32 [320, 64, 512], P(None, ('groups', 'cols'), 'rows'), parts along dimension 1
- control_out: float32 [320, 64, 512], P(None, ('groups', 'cols', 'rows')), parts along dimension 1
There are 2 independent parts, one for each index of `groups`. A program takes and returns all parts, laid end to end along the dimension named above; an argument that names none is the same for every part. Nothing has to cross between parts.
All inputs are finite; a program needn't handle non-finite values.
Results may differ from a plain program's by a relative error of at most 0.0033.
Values may be sent and summed in bfloat16 or wider, within the bound.
A program may use at most 64 MiB of HBM per device.

v0:
```python
import jax
import jax.numpy as jnp
from jax import lax
from jax.sharding import PartitionSpec as P


def padded_2(value, sides, width):
    for axis, dim in sides:
        count, length = (lax.axis_size(axis), value.shape[dim])
        up = [(i, (i + 1) % count) for i in range(count - 1)]
        down = [(j, i) for i, j in up]
        last = lax.slice_in_dim(value, length - width, length, axis=dim)
        leading = lax.slice_in_dim(value, 0, width, axis=dim)
        before = lax.ppermute(last, axis, up)
        after = lax.ppermute(leading, axis, down)
        value = jnp.concatenate([before, value, after], axis=dim)
    return value


def convolve(padded, weight, bias):
    width = padded.shape[1] - 2
    height = padded.shape[2] - 2
    total = jnp.zeros((weight.shape[1], width, height), jnp.float32)
    for offset in range(9):
        across = offset // 3
        down = offset % 3
        window = padded[:, across : across + width, down : down + height]
        total = total + jnp.einsum(
            "oc,cwh->owh", weight[offset], window, preferred_element_type=jnp.float32
        )
    return total + bias[:, None, None]


def project(matrix, field):
    return jnp.einsum("oc,cwh->owh", matrix, field, preferred_element_type=jnp.float32)


def per_device(
    base_field,
    control_field,
    first_kernel,
    second_kernel,
    control_kernel,
    first_bias,
    second_bias,
    control_bias,
    to_control,
    to_base,
):
    base_round = base_field.astype(jnp.bfloat16)
    tile_cols = base_field.shape[1]
    tile_rows = base_field.shape[2]
    padded = padded_2(base_round, (("cols", 1), ("rows", 2)), 2)
    inner = jax.nn.silu(convolve(padded, first_kernel, first_bias))
    across = lax.axis_index("cols") * tile_cols - 1 + jnp.arange(tile_cols + 2, dtype=jnp.int32)
    downward = lax.axis_index("rows") * tile_rows - 1 + jnp.arange(tile_rows + 2, dtype=jnp.int32)
    col_inside = (across >= 0) & (across < tile_cols * lax.axis_size("cols"))
    row_inside = (downward >= 0) & (downward < tile_rows * lax.axis_size("rows"))
    inside = col_inside[:, None] & row_inside[None, :]
    hidden_ext = jnp.where(inside[None], inner, 0.0).astype(jnp.bfloat16)
    base_mid = jax.nn.silu(convolve(hidden_ext, second_kernel, second_bias)) + base_field
    base_send = base_mid.astype(jnp.bfloat16)
    control_round = control_field.astype(jnp.bfloat16)
    edged = padded_2(control_round, ((("cols", "rows"), 1),), 1)
    edged = jnp.pad(edged, ((0, 0), (0, 0), (1, 1)))
    control_mid = jax.nn.silu(convolve(edged, control_kernel, control_bias)) + control_field
    arrived = lax.all_to_all(base_send, "rows", split_axis=1, concat_axis=2, tiled=True)
    control_out = control_mid + project(to_control, arrived)
    control_send = control_out.astype(jnp.bfloat16)
    returned = lax.all_to_all(control_send, "rows", split_axis=2, concat_axis=1, tiled=True)
    base_out = base_mid + project(to_base, returned)
    return (base_out, control_out)


def solution(mesh):
    return jax.shard_map(
        per_device,
        mesh=mesh,
        in_specs=(
            P(None, ("groups", "cols"), "rows"),
            P(None, ("groups", "cols", "rows"), None),
            P(),
            P(),
            P(),
            P(),
            P(),
            P(),
            P(),
            P(),
        ),
        out_specs=(P(None, ("groups", "cols"), "rows"), P(None, ("groups", "cols", "rows"), None)),
        check_vma=False,
    )
```

profile of v0, /device:TPU:0, one launch (start us, length us, event | category | flops | bytes accessed | tf_op | source)
XLA Modules:
  0.0 80.0 jit_solution(4251604718525200333)
XLA Ops:
  0.7 1.8 %copy.29 = bf16[320,8,128]{0,2,1:T(8,128)(2,1)S(1)} copy(f32[320,8,128]{2,1,0:T(8,128)} %param.10) | data formatting | bytes 1966080 | tf_op args[0]
  2.5 0.8 fusion.120
  3.3 1.3 %collective-permute-start.1 = (bf16[320,2,128]{0,2,1:T(8,128)(2,1)}, bf16[320,2,128]{0,2,1:T(8,128)(2,1)S(1)}, u32[]{:S(2)}, u32[]{:S(2)}) collective-permute-start(bf16[320,2,128]{0,2,1:T(8,128)(2,1)} %get-tuple-element.9), channel_id=1, source_target_pairs={{4,0},{8,4},{12,8},{5,1},{9,5},{13,9},{6,2},{10,6},{14,10},{7,3},{... | collective-permute-start | bytes 491528 | tf_op jit(solution)/shard_map/ppermute | solution.py:15
  4.5 5.6 %collective-permute-start = (bf16[320,2,128]{0,2,1:T(8,128)(2,1)}, bf16[320,2,128]{0,2,1:T(8,128)(2,1)S(1)}, u32[]{:S(2)}, u32[]{:S(2)}) collective-permute-start(bf16[320,2,128]{0,2,1:T(8,128)(2,1)} %get-tuple-element.8), channel_id=1, source_target_pairs={{0,4},{4,8},{8,12},{1,5},{5,9},{9,13},{2,6},{6,10},{10,14},{3,7},{... | collective-permute-start | bytes 491528 | tf_op jit(solution)/shard_map/ppermute | solution.py:14
  10.4 0.9 %fusion.121 = (bf16[320,1,512]{2,0,1:T(8,128)(2,1)}, bf16[320,1,512]{2,0,1:T(8,128)(2,1)}) fusion(bf16[320,2,512]{2,0,1:T(8,128)(2,1)S(1)} %copy.64), kind=kLoop, calls=%fused_computation.151 | loop fusion | bytes 1310720 | tf_op jit(solution)/shard_map/slice | solution.py:12
  11.2 1.3 %collective-permute-start.5 = (bf16[320,1,512]{2,0,1:T(8,128)(2,1)}, bf16[320,1,512]{2,0,1:T(8,128)(2,1)}, u32[]{:S(2)}, u32[]{:S(2)}) collective-permute-start(bf16[320,1,512]{2,0,1:T(8,128)(2,1)} %get-tuple-element.11), channel_id=1, source_target_pairs={{1,0},{2,1},{3,2},{4,3},{5,4},{6,5},{7,6},{8,7},{9,8},{10,9},{11,1... | collective-permute-start | bytes 983048 | tf_op jit(solution)/shard_map/ppermute | solution.py:15
  12.5 3.8 %collective-permute-start.4 = (bf16[320,1,512]{2,0,1:T(8,128)(2,1)}, bf16[320,1,512]{2,0,1:T(8,128)(2,1)}, u32[]{:S(2)}, u32[]{:S(2)}) collective-permute-start(bf16[320,1,512]{2,0,1:T(8,128)(2,1)} %get-tuple-element.10), channel_id=1, source_target_pairs={{0,1},{1,2},{2,3},{3,4},{4,5},{5,6},{6,7},{7,8},{8,9},{9,10},{10,1... | collective-permute-start | bytes 983048 | tf_op jit(solution)/shard_map/ppermute | solution.py:14
  16.3 1.4 %fusion.59 = f32[320,2,512]{2,0,1:T(8,128)S(1)} fusion(bf16[320,2,512]{2,0,1:T(8,128)(2,1)S(1)} %copy.64, bf16[9,320,320]{2,1,0:T(8,128)(2,1)} %param.14), kind=kOutput, calls=%fused_computation.85 | convolution fusion | flops 209715200 | bytes 2211840 | tf_op jit(solution)/shard_map/oc,cwh->owh/dot_general | solution.py:28
  17.8 1.4 %collective-permute-start.3 = (bf16[320,12,2]{0,2,1:T(2,128)(2,1)S(1)}, bf16[320,12,2]{0,2,1:T(2,128)(2,1)S(1)}, u32[]{:S(2)}, u32[]{:S(2)}) collective-permute-start(bf16[320,12,2]{0,2,1:T(2,128)(2,1)S(1)} %get-tuple-element.7), channel_id=1, source_target_pairs={{1,0},{2,1},{3,2},{5,4},{6,5},{7,6},{9,8},{10,9},{11,10},{13,12},{... | collective-permute-start | bytes 46088 | tf_op jit(solution)/shard_map/ppermute | solution.py:15
  19.3 3.4 %collective-permute-start.2 = (bf16[320,12,2]{0,2,1:T(2,128)(2,1)S(1)}, bf16[320,12,2]{0,2,1:T(2,128)(2,1)S(1)}, u32[]{:S(2)}, u32[]{:S(2)}) collective-permute-start(bf16[320,12,2]{0,2,1:T(2,128)(2,1)S(1)} %get-tuple-element.6), channel_id=1, source_target_pairs={{0,1},{1,2},{2,3},{4,5},{5,6},{6,7},{8,9},{9,10},{10,11},{12,13},{... | collective-permute-start | bytes 46088 | tf_op jit(solution)/shard_map/ppermute | solution.py:14
  24.0 0.8 %fusion.24 = f32[10,130,320]{2,1,0:T(8,128)S(1)} fusion(bf16[320,12,132]{0,2,1:T(8,128)(2,1)S(1)} %pad_maximum_fusion, bf16[9,320,320]{2,1,0:T(8,128)(2,1)S(1)} %copy-done.5), kind=kOutput, calls=%fused_computation.48 | convolution fusion | flops 266240000 | bytes 2954240 | tf_op jit(solution)/shard_map/oc,cwh->owh/dot_general | solution.py:28
  24.8 0.8 %fusion.26 = f32[10,130,320]{2,1,0:T(8,128)S(1)} fusion(bf16[320,12,132]{0,2,1:T(8,128)(2,1)S(1)} %pad_maximum_fusion, bf16[9,320,320]{2,1,0:T(8,128)(2,1)S(1)} %copy-done.5), kind=kOutput, calls=%fused_computation.50 | convolution fusion | flops 266240000 | bytes 2954240 | tf_op jit(solution)/shard_map/oc,cwh->owh/dot_general | solution.py:28
  25.6 0.8 %fusion.28 = f32[10,130,320]{2,1,0:T(8,128)S(1)} fusion(bf16[320,12,132]{0,2,1:T(8,128)(2,1)S(1)} %pad_maximum_fusion, bf16[9,320,320]{2,1,0:T(8,128)(2,1)S(1)} %copy-done.5), kind=kOutput, calls=%fused_computation.52 | convolution fusion | flops 266240000 | bytes 2954240 | tf_op jit(solution)/shard_map/oc,cwh->owh/dot_general | solution.py:28
  26.4 0.8 %fusion.79 = f32[10,130,320]{2,1,0:T(8,128)S(1)} fusion(bf16[9,320,320]{2,1,0:T(8,128)(2,1)S(1)} %copy-done.5, bf16[320,2,128]{0,2,1:T(8,128)(2,1)S(1)} %collective-permute-done.1, bf16[320,8,128]{0,2,1:T(8,128)(2,1)S(1)} %copy.29, bf16[320,2,128]{0,2,1:T(8,128)(2,1)S(1)} %collective-permute-done, bf16[320,12,2]{0,2,1:T(2,128)(2,1)S(1)} %collective-permute-done.2), kind=kOutput, calls=%fused_computation.103 | convolution fusion | flops 270233600 | bytes 3107840 | tf_op jit(solution)/shard_map/oc,cwh->owh/dot_general | solution.py:28
  27.2 0.8 fusion.81
  28.0 0.8 %fusion.84 = f32[10,130,320]{2,1,0:T(8,128)S(1)} fusion(bf16[9,320,320]{2,1,0:T(8,128)(2,1)S(1)} %copy-done.5, bf16[320,2,128]{0,2,1:T(8,128)(2,1)S(1)} %collective-permute-done.1, bf16[320,8,128]{0,2,1:T(8,128)(2,1)S(1)} %copy.29, bf16[320,2,128]{0,2,1:T(8,128)(2,1)S(1)} %collective-permute-done, bf16[320,12,2]{0,2,1:T(2,128)(2,1)S(1)} %collective-permute-done.2), kind=kOutput, calls=%fused_computation.108 | convolution fusion | flops 270233600 | bytes 3107840 | tf_op jit(solution)/shard_map/oc,cwh->owh/dot_general | solution.py:28
  28.8 0.8 fusion.86
  29.7 0.8 %fusion.89 = f32[10,130,320]{2,1,0:T(8,128)S(1)} fusion(bf16[9,320,320]{2,1,0:T(8,128)(2,1)S(1)} %copy-done.5, bf16[320,2,128]{0,2,1:T(8,128)(2,1)S(1)} %collective-permute-done.1, bf16[320,8,128]{0,2,1:T(8,128)(2,1)S(1)} %copy.29, bf16[320,2,128]{0,2,1:T(8,128)(2,1)S(1)} %collective-permute-done, bf16[320,12,2]{0,2,1:T(2,128)(2,1)S(1)} %collective-permute-done.2), kind=kOutput, calls=%fused_computation.113 | convolution fusion | flops 270233600 | bytes 3107840 | tf_op jit(solution)/shard_map/oc,cwh->owh/dot_general | solution.py:28
  30.5 2.3 %fusion.5 = bf16[320,10,130]{0,2,1:T(8,128)(2,1)S(1)} fusion(f32[10,130,320]{2,1,0:T(8,128)S(1)} %fusion.24, f32[10,130,320]{2,1,0:T(8,128)S(1)} %fusion.79, f32[10,130,320]{2,1,0:T(8,128)S(1)} %fusion.81, f32[10,130,320]{2,1,0:T(8,128)S(1)} %fusion.26, f32[10,130,320]{2,1,0:T(8,128)S(1)} %fusion.84, f32[10,130,320]{2,1,0:T(8,128)S(1)} %fusion.86, ...), kind=kOutput, calls=%fused_computation.9 | convolution fusion | flops 276473600 | bytes 18993664 | tf_op jit(solution)/shard_map/oc,cwh->owh/dot_general | solution.py:28
  38.0 1.7 %fusion.122 = (bf16[320,8,128]{2,0,1:T(8,128)(2,1)}, f32[320,8,128]{2,0,1:T(8,128)S(1)}) fusion(f32[320,8,128]{2,1,0:T(8,128)S(1)} %copy-done.3, f32[320]{0:T(512)S(1)} %copy-done.9, f32[8,128,320]{1,2,0:T(8,128)S(1)} %convolution_add_fusion.2, bf16[9,320,320]{2,1,0:T(8,128)(2,1)S(1)} %copy-done.2, bf16[320,10,130]{0,2,1:T(8,128)(2,1)S(1)} %fusion.5), kind=kOutput, calls=%fused_computation.152 | convolution fusion | flops 212336640 | bytes 5621760 | tf_op jit(solution)/shard_map/oc,cwh->owh/dot_general | solution.py:28
  39.8 5.2 %all-to-all-start = ((bf16[320,8,128]{2,0,1:T(8,128)(2,1)}), bf16[320,8,128]{2,0,1:T(8,128)(2,1)}, u32[]{:S(2)}, u32[]{:S(2)}) async-start(bf16[320,8,128]{2,0,1:T(8,128)(2,1)} %get-tuple-element.12), calls=%async_computation | async-start | bytes 1310720 | tf_op jit(solution)/shard_map/all_to_all | solution.py:67
  45.0 2.1 %fusion.10 = bf16[320,4,514]{2,0,1:T(8,128)(2,1)S(1)} fusion(bf16[320,1,512]{2,0,1:T(8,128)(2,1)} %collective-permute-done.5, bf16[320,2,512]{2,0,1:T(8,128)(2,1)S(1)} %copy.64, bf16[320,1,512]{2,0,1:T(8,128)(2,1)} %collective-permute-done.4), kind=kLoop, calls=%fused_computation.14 | loop fusion | flops 7895040 | bytes 2626560 | tf_op jit(solution)/shard_map/concatenate | solution.py:16
  50.0 1.5 %convolution_bitcast_fusion.3 = f32[320,2,512]{2,0,1:T(8,128)S(1)} fusion(bf16[320,1,512]{2,0,1:T(8,128)(2,1)} %collective-permute-done.5, bf16[320,2,512]{2,0,1:T(8,128)(2,1)S(1)} %copy.64, bf16[9,320,320]{2,1,0:T(8,128)(2,1)S(1)} %copy-done.1), kind=kOutput, calls=%fused_computation.38 | convolution fusion | flops 211025920 | bytes 2539520 | tf_op jit(solution)/shard_map/oc,cwh->owh/dot_general | solution.py:28
  51.5 1.5 %fusion.50 = f32[2,512,320]{1,2,0:T(8,128)S(1)} fusion(bf16[320,2,512]{2,0,1:T(8,128)(2,1)S(1)} %copy.64, bf16[320,1,512]{2,0,1:T(8,128)(2,1)} %collective-permute-done.4, bf16[9,320,320]{2,1,0:T(8,128)(2,1)S(1)} %copy-done.1), kind=kOutput, calls=%fused_computation.76 | convolution fusion | flops 211025920 | bytes 2539520 | tf_op jit(solution)/shard_map/oc,cwh->owh/dot_general | solution.py:28
  53.0 1.9 %fusion.23 = f32[320,2,512]{2,0,1:T(8,128)} fusion(f32[320,2,512]{2,0,1:T(8,128)S(1)} %convolution_bitcast_fusion.2, f32[320,2,512]{2,0,1:T(8,128)S(1)} %convolution_bitcast_fusion.3, f32[320,2,512]{2,0,1:T(8,128)S(1)} %convolution_bitcast_fusion.4, f32[320,2,512]{2,0,1:T(8,128)S(1)} %convolution_bitcast_fusion.5, f32[320,2,512]{2,0,1:T(8,128)S(1)} %fusion.59, ...), kind=kOutput, calls=%fused_computation.42 | convolution fusion | flops 212664320 | bytes 12699648 | tf_op jit(solution)/shard_map/oc,cwh->owh/dot_general | solution.py:28
  55.3 3.7 %fusion.123 = (bf16[320,2,512]{2,0,1:T(8,128)(2,1)S(1)}, f32[320,2,512]{2,0,1:T(8,128)}) fusion(bf16[4,2,40,8,128]{4,3,2,1,0:T(8,128)(2,1)} %bitcast.72, bf16[320,320]{1,0:T(8,128)(2,1)S(1)} %copy-done, f32[320,2,512]{2,1,0:T(2,128)} %param.11, f32[320,2,512]{2,0,1:T(8,128)} %fusion.23), kind=kOutput, calls=%fused_computation.153 | convolution fusion | flops 212008960 | bytes 5447680 | tf_op jit(solution)/shard_map/oc,cwh->owh/dot_general | solution.py:35
  59.0 1.9 %copy.43 = bf16[320,2,512]{0,1,2:T(2,128)(2,1)} copy(bf16[320,2,512]{2,0,1:T(8,128)(2,1)S(1)} %get-tuple-element.14) | data formatting | bytes 1310720 | tf_op jit(solution)/shard_map/convert_element_type | solution.py:69
  60.8 4.0 %all-to-all-start.1 = ((bf16[320,2,512]{0,1,2:T(2,128)(2,1)}), bf16[320,2,512]{0,1,2:T(2,128)(2,1)S(1)}, u32[]{:S(2)}, u32[]{:S(2)}) async-start(bf16[320,2,512]{0,1,2:T(2,128)(2,1)} %copy.43), calls=%async_computation.1 | async-start | bytes 1572864 | tf_op jit(solution)/shard_map/all_to_all | solution.py:70
  64.8 3.4 %copy.46 = f32[320,2,512]{2,1,0:T(2,128)} copy(f32[320,2,512]{2,0,1:T(8,128)} %get-tuple-element.15) | data formatting | bytes 2621440
  68.3 8.2 %all-to-all-done.1 = bf16[320,2,512]{0,1,2:T(2,128)(2,1)S(1)} async-done(((bf16[320,2,512]{0,1,2:T(2,128)(2,1)}), bf16[320,2,512]{0,1,2:T(2,128)(2,1)S(1)}, u32[]{:S(2)}, u32[]{:S(2)}) %all-to-all-start.1) | async-done | bytes 655392 | tf_op jit(solution)/shard_map/all_to_all | solution.py:70
  76.4 1.2 %copy.44 = bf16[320,2,4,128]{3,0,1,2:T(8,128)(2,1)S(1)} copy(bf16[320,2,4,128]{0,1,3,2:T(2,128)(2,1)S(1)} %bitcast.184) | data formatting | bytes 1310720 | tf_op jit(solution)/shard_map/all_to_all | solution.py:70
  78.2 1.8 %copy.45 = f32[320,8,128]{2,1,0:T(8,128)} copy(f32[320,8,128]{2,0,1:T(8,128)S(1)} %fusion.20) | data formatting | bytes 2621440
  (47 shorter events, 10.4 us)
Async XLA Ops:
  0.6 54.7 %copy-start = (bf16[320,320]{1,0:T(8,128)(2,1)S(1)}, bf16[320,320]{1,0:T(8,128)(2,1)}, u32[]{:S(2)}) copy-start(bf16[320,320]{1,0:T(8,128)(2,1)} %param.18) | copy-start | bytes 614404
  0.6 9.5 %copy-start.4 = (f32[320,2,512]{2,1,0:T(2,128)S(1)}, f32[320,2,512]{2,1,0:T(2,128)}, u32[]{:S(2)}) copy-start(f32[320,2,512]{2,1,0:T(2,128)} %param.11) | copy-start | bytes 3932164
  3.3 14.5 %collective-permute-start.1 = (bf16[320,2,128]{0,2,1:T(8,128)(2,1)}, bf16[320,2,128]{0,2,1:T(8,128)(2,1)S(1)}, u32[]{:S(2)}, u32[]{:S(2)}) collective-permute-start(bf16[320,2,128]{0,2,1:T(8,128)(2,1)} %get-tuple-element.9), channel_id=1, source_target_pairs={{4,0},{8,4},{12,8},{5,1},{9,5},{13,9},{6,2},{10,6},{14,10},{7,3},{... | collective-permute-start | bytes 491528 | tf_op jit(solution)/shard_map/ppermute | solution.py:15
  4.5 13.2 %collective-permute-start = (bf16[320,2,128]{0,2,1:T(8,128)(2,1)}, bf16[320,2,128]{0,2,1:T(8,128)(2,1)S(1)}, u32[]{:S(2)}, u32[]{:S(2)}) collective-permute-start(bf16[320,2,128]{0,2,1:T(8,128)(2,1)} %get-tuple-element.8), channel_id=1, source_target_pairs={{0,4},{4,8},{8,12},{1,5},{5,9},{9,13},{2,6},{6,10},{10,14},{3,7},{... | collective-permute-start | bytes 491528 | tf_op jit(solution)/shard_map/ppermute | solution.py:14
  11.2 33.7 %collective-permute-start.5 = (bf16[320,1,512]{2,0,1:T(8,128)(2,1)}, bf16[320,1,512]{2,0,1:T(8,128)(2,1)}, u32[]{:S(2)}, u32[]{:S(2)}) collective-permute-start(bf16[320,1,512]{2,0,1:T(8,128)(2,1)} %get-tuple-element.11), channel_id=1, source_target_pairs={{1,0},{2,1},{3,2},{4,3},{5,4},{6,5},{7,6},{8,7},{9,8},{10,9},{11,1... | collective-permute-start | bytes 983048 | tf_op jit(solution)/shard_map/ppermute | solution.py:15
  12.5 32.5 %collective-permute-start.4 = (bf16[320,1,512]{2,0,1:T(8,128)(2,1)}, bf16[320,1,512]{2,0,1:T(8,128)(2,1)}, u32[]{:S(2)}, u32[]{:S(2)}) collective-permute-start(bf16[320,1,512]{2,0,1:T(8,128)(2,1)} %get-tuple-element.10), channel_id=1, source_target_pairs={{0,1},{1,2},{2,3},{3,4},{4,5},{5,6},{6,7},{7,8},{8,9},{9,10},{10,1... | collective-permute-start | bytes 983048 | tf_op jit(solution)/shard_map/ppermute | solution.py:14
  17.8 6.2 %copy-start.5 = (bf16[9,320,320]{2,1,0:T(8,128)(2,1)S(1)}, bf16[9,320,320]{2,1,0:T(8,128)(2,1)}, u32[]{:S(2)}) copy-start(bf16[9,320,320]{2,1,0:T(8,128)(2,1)} %param.12) | copy-start | bytes 5529604
  17.8 4.9 %collective-permute-start.3 = (bf16[320,12,2]{0,2,1:T(2,128)(2,1)S(1)}, bf16[320,12,2]{0,2,1:T(2,128)(2,1)S(1)}, u32[]{:S(2)}, u32[]{:S(2)}) collective-permute-start(bf16[320,12,2]{0,2,1:T(2,128)(2,1)S(1)} %get-tuple-element.7), channel_id=1, source_target_pairs={{1,0},{2,1},{3,2},{5,4},{6,5},{7,6},{9,8},{10,9},{11,10},{13,12},{... | collective-permute-start | bytes 46088 | tf_op jit(solution)/shard_map/ppermute | solution.py:15
  19.3 4.2 %collective-permute-start.2 = (bf16[320,12,2]{0,2,1:T(2,128)(2,1)S(1)}, bf16[320,12,2]{0,2,1:T(2,128)(2,1)S(1)}, u32[]{:S(2)}, u32[]{:S(2)}) collective-permute-start(bf16[320,12,2]{0,2,1:T(2,128)(2,1)S(1)} %get-tuple-element.6), channel_id=1, source_target_pairs={{0,1},{1,2},{2,3},{4,5},{5,6},{6,7},{8,9},{9,10},{10,11},{12,13},{... | collective-permute-start | bytes 46088 | tf_op jit(solution)/shard_map/ppermute | solution.py:14
  29.6 0.8 %copy-start.8 = (f32[320]{0:T(512)S(1)}, f32[320]{0:T(512)}, u32[]{:S(2)}) copy-start(f32[320]{0:T(512)} %param.15) | copy-start | bytes 3844
  30.5 2.4 %copy-start.2 = (bf16[9,320,320]{2,1,0:T(8,128)(2,1)S(1)}, bf16[9,320,320]{2,1,0:T(8,128)(2,1)}, u32[]{:S(2)}) copy-start(bf16[9,320,320]{2,1,0:T(8,128)(2,1)} %param.13) | copy-start | bytes 5529604
  36.7 1.3 %copy-start.3 = (f32[320,8,128]{2,1,0:T(8,128)S(1)}, f32[320,8,128]{2,1,0:T(8,128)}, u32[]{:S(2)}) copy-start(f32[320,8,128]{2,1,0:T(8,128)} %param.10) | copy-start | bytes 3932164
  36.7 1.3 %copy-start.9 = (f32[320]{0:T(512)S(1)}, f32[320]{0:T(512)}, u32[]{:S(2)}) copy-start(f32[320]{0:T(512)} %param.16) | copy-start | bytes 3844
  39.8 15.5 %all-to-all-start = ((bf16[320,8,128]{2,0,1:T(8,128)(2,1)}), bf16[320,8,128]{2,0,1:T(8,128)(2,1)}, u32[]{:S(2)}, u32[]{:S(2)}) async-start(bf16[320,8,128]{2,0,1:T(8,128)(2,1)} %get-tuple-element.12), calls=%async_computation | async-start | bytes 1310720 | tf_op jit(solution)/shard_map/all_to_all | solution.py:67
  45.0 2.1 %copy-start.1 = (bf16[9,320,320]{2,1,0:T(8,128)(2,1)S(1)}, bf16[9,320,320]{2,1,0:T(8,128)(2,1)}, u32[]{:S(2)}) copy-start(bf16[9,320,320]{2,1,0:T(8,128)(2,1)} %param.14) | copy-start | bytes 5529604
  51.5 1.5 %copy-start.7 = (f32[320]{0:T(512)S(1)}, f32[320]{0:T(512)}, u32[]{:S(2)}) copy-start(f32[320]{0:T(512)} %param.17) | copy-start | bytes 3844
  60.8 15.6 %all-to-all-start.1 = ((bf16[320,2,512]{0,1,2:T(2,128)(2,1)}), bf16[320,2,512]{0,1,2:T(2,128)(2,1)S(1)}, u32[]{:S(2)}, u32[]{:S(2)}) async-start(bf16[320,2,512]{0,1,2:T(2,128)(2,1)} %copy.43), calls=%async_computation.1 | async-start | bytes 1572864 | tf_op jit(solution)/shard_map/all_to_all | solution.py:70
  64.8 12.8 %copy-start.6 = (bf16[320,320]{1,0:T(8,128)(2,1)S(1)}, bf16[320,320]{1,0:T(8,128)(2,1)}, u32[]{:S(2)}) copy-start(bf16[320,320]{1,0:T(8,128)(2,1)} %param.19) | copy-start | bytes 614404
where the time goes:
time: 80.5 us; the launch traced here: 80 us
  matrix products  28.2 us (35%)
  starting transfers between devices  25.9 us (32%)
  local copies, waits for them, and re-layouts  12.8 us (16%)
  waiting for transfers between devices  9.34 us (12%)
  other arithmetic  2.73 us (3%)
  between operations  1.07 us (1%)
    dot_general x27, matrix products, convolve(): jnp.einsum('oc,cwh->owh', weight[offset], window, preferred_element_type=...  24 us
    ppermute x3, starting transfers between devices, padded_2(): before = lax.ppermute(last, axis, up)  12.7 us
    all_to_all x1, waiting for transfers between devices, per_device(): lax.all_to_all(control_send, 'rows', split_axis=2, concat_axis=1, tiled=T...  8.19 us
    unnamed x24, local copies, waits for them, and re-layouts  8.05 us
    all_to_all x1, starting transfers between devices, per_device(): lax.all_to_all(base_send, 'rows', split_axis=1, concat_axis=2, tiled=True)  5.23 us
    dot_general x2, matrix products, project(): jnp.einsum('oc,cwh->owh', matrix, field, preferred_element_type=jnp.float32)  4.17 us
    all_to_all x1, starting transfers between devices, per_device(): lax.all_to_all(control_send, 'rows', split_axis=2, concat_axis=1, tiled=T...  3.99 us
    ppermute x3, starting transfers between devices, padded_2(): after = lax.ppermute(leading, axis, down)  3.98 us
  transfers between devices with their start and end apart: 8, of which 3 were waited for; matrix products, arithmetic and copies ran while one was open for 39% of the time, Pallas kernels for 0%

commit v1 on v0

--- a/solution.py
+++ b/solution.py
@@ -67,7 +67,10 @@
     arrived = lax.all_to_all(base_send, "rows", split_axis=1, concat_axis=2, tiled=True)
     control_out = control_mid + project(to_control, arrived)
     control_send = control_out.astype(jnp.bfloat16)
-    returned = lax.all_to_all(control_send, "rows", split_axis=2, concat_axis=1, tiled=True)
+    size = lax.axis_size("rows")
+    blocks = jnp.stack(jnp.split(control_send, size, axis=2), axis=0)
+    blocks = lax.all_to_all(blocks, "rows", split_axis=0, concat_axis=0)
+    returned = jnp.concatenate(blocks, axis=1)
     base_out = base_mid + project(to_base, returned)
     return (base_out, control_out)
 

time: 80.5 us -> 77 us (0.957)
  local copies, waits for them, and re-layouts: 12.8 us -> 8.47 us
  other arithmetic: 2.73 us -> 3.65 us
    convert_element_type x1 -> x0, local copies, waits for them, and re-layouts: 1.86 us -> none  [per_device(): control_send = control_out.astype(jnp.bfloat16)]
    unnamed x24 -> x22, local copies, waits for them, and re-layouts: 8.05 us -> 6.69 us
    all_to_all x1 -> x0, local copies, waits for them, and re-layouts: 1.18 us -> none  [per_device(): lax.all_to_all(control_send, 'rows', split_axis=2, concat_axis=1, tiled=T...]
    another operation x0 -> x1, other arithmetic: none -> 0.92 us  [per_device(): blocks = jnp.stack(jnp.split(control_send, size, axis=2), axis=0)]
where the time goes in v1:
time: 77 us; the launch traced here: 76.5 us
  matrix products  28 us (36%)
  starting transfers between devices  25.9 us (34%)
  waiting for transfers between devices  9.29 us (12%)
  local copies, waits for them, and re-layouts  8.47 us (11%)
  other arithmetic  3.65 us (5%)
  between operations  1.07 us (1%)
    dot_general x27, matrix products, convolve(): jnp.einsum('oc,cwh->owh', weight[offset], window, preferred_element_type=...  24 us
    ppermute x3, starting transfers between devices, padded_2(): before = lax.ppermute(last, axis, up)  12.7 us
    all_to_all x1, waiting for transfers between devices, per_device(): blocks = lax.all_to_all(blocks, 'rows', split_axis=0, concat_axis=0)  8.15 us
    unnamed x22, local copies, waits for them, and re-layouts  6.69 us
    all_to_all x1, starting transfers between devices, per_device(): lax.all_to_all(base_send, 'rows', split_axis=1, concat_axis=2, tiled=True)  5.23 us
    dot_general x2, matrix products, project(): jnp.einsum('oc,cwh->owh', matrix, field, preferred_element_type=jnp.float32)  4.05 us
    all_to_all x1, starting transfers between devices, per_device(): blocks = lax.all_to_all(blocks, 'rows', split_axis=0, concat_axis=0)  3.99 us
    ppermute x3, starting transfers between devices, padded_2(): after = lax.ppermute(leading, axis, down)  3.98 us
  transfers between devices with their start and end apart: 8, of which 3 were waited for; matrix products, arithmetic and copies ran while one was open for 39% of the time, Pallas kernels for 0%

profile of v1, /device:TPU:0, one launch (start us, length us, event | category | flops | bytes accessed | tf_op | source)
XLA Modules:
  0.0 76.5 jit_solution(6459789452707213470)
XLA Ops:
  0.7 1.8 %copy.12 = bf16[320,8,128]{0,2,1:T(8,128)(2,1)S(1)} copy(f32[320,8,128]{2,1,0:T(8,128)} %param.10) | data formatting | bytes 1966080 | tf_op args[0]
  2.5 0.8 %fusion.120 = (bf16[320,2,128]{0,2,1:T(8,128)(2,1)}, bf16[320,2,128]{0,2,1:T(8,128)(2,1)}) fusion(bf16[320,8,128]{0,2,1:T(8,128)(2,1)S(1)} %copy.12), kind=kLoop, calls=%fused_computation.155 | loop fusion | bytes 655360 | tf_op jit(solution)/shard_map/slice | solution.py:12
  3.3 1.3 %collective-permute-start.1 = (bf16[320,2,128]{0,2,1:T(8,128)(2,1)}, bf16[320,2,128]{0,2,1:T(8,128)(2,1)S(1)}, u32[]{:S(2)}, u32[]{:S(2)}) collective-permute-start(bf16[320,2,128]{0,2,1:T(8,128)(2,1)} %get-tuple-element.7), channel_id=1, source_target_pairs={{4,0},{8,4},{12,8},{5,1},{9,5},{13,9},{6,2},{10,6},{14,10},{7,3},{... | collective-permute-start | bytes 491528 | tf_op jit(solution)/shard_map/ppermute | solution.py:15
  4.5 5.6 %collective-permute-start = (bf16[320,2,128]{0,2,1:T(8,128)(2,1)}, bf16[320,2,128]{0,2,1:T(8,128)(2,1)S(1)}, u32[]{:S(2)}, u32[]{:S(2)}) collective-permute-start(bf16[320,2,128]{0,2,1:T(8,128)(2,1)} %get-tuple-element.6), channel_id=1, source_target_pairs={{0,4},{4,8},{8,12},{1,5},{5,9},{9,13},{2,6},{6,10},{10,14},{3,7},{... | collective-permute-start | bytes 491528 | tf_op jit(solution)/shard_map/ppermute | solution.py:14
  10.4 0.9 %fusion.121 = (bf16[320,1,512]{2,0,1:T(8,128)(2,1)}, bf16[320,1,512]{2,0,1:T(8,128)(2,1)}) fusion(bf16[320,2,512]{2,0,1:T(8,128)(2,1)S(1)} %copy.45), kind=kLoop, calls=%fused_computation.156 | loop fusion | bytes 1310720 | tf_op jit(solution)/shard_map/slice | solution.py:12
  11.2 1.3 %collective-permute-start.5 = (bf16[320,1,512]{2,0,1:T(8,128)(2,1)}, bf16[320,1,512]{2,0,1:T(8,128)(2,1)}, u32[]{:S(2)}, u32[]{:S(2)}) collective-permute-start(bf16[320,1,512]{2,0,1:T(8,128)(2,1)} %get-tuple-element.13), channel_id=1, source_target_pairs={{1,0},{2,1},{3,2},{4,3},{5,4},{6,5},{7,6},{8,7},{9,8},{10,9},{11,1... | collective-permute-start | bytes 983048 | tf_op jit(solution)/shard_map/ppermute | solution.py:15
  12.5 3.8 %collective-permute-start.4 = (bf16[320,1,512]{2,0,1:T(8,128)(2,1)}, bf16[320,1,512]{2,0,1:T(8,128)(2,1)}, u32[]{:S(2)}, u32[]{:S(2)}) collective-permute-start(bf16[320,1,512]{2,0,1:T(8,128)(2,1)} %get-tuple-element.12), channel_id=1, source_target_pairs={{0,1},{1,2},{2,3},{3,4},{4,5},{5,6},{6,7},{7,8},{8,9},{9,10},{10,1... | collective-permute-start | bytes 983048 | tf_op jit(solution)/shard_map/ppermute | solution.py:14
  16.3 1.4 %fusion.59 = f32[320,2,512]{2,0,1:T(8,128)S(1)} fusion(bf16[320,2,512]{2,0,1:T(8,128)(2,1)S(1)} %copy.45, bf16[9,320,320]{2,1,0:T(8,128)(2,1)} %param.14), kind=kOutput, calls=%fused_computation.86 | convolution fusion | flops 209715200 | bytes 2211840 | tf_op jit(solution)/shard_map/oc,cwh->owh/dot_general | solution.py:28
  17.8 1.4 %collective-permute-start.3 = (bf16[320,12,2]{0,2,1:T(2,128)(2,1)S(1)}, bf16[320,12,2]{0,2,1:T(2,128)(2,1)S(1)}, u32[]{:S(2)}, u32[]{:S(2)}) collective-permute-start(bf16[320,12,2]{0,2,1:T(2,128)(2,1)S(1)} %get-tuple-element.5), channel_id=1, source_target_pairs={{1,0},{2,1},{3,2},{5,4},{6,5},{7,6},{9,8},{10,9},{11,10},{13,12},{... | collective-permute-start | bytes 46088 | tf_op jit(solution)/shard_map/ppermute | solution.py:15
  19.3 3.4 %collective-permute-start.2 = (bf16[320,12,2]{0,2,1:T(2,128)(2,1)S(1)}, bf16[320,12,2]{0,2,1:T(2,128)(2,1)S(1)}, u32[]{:S(2)}, u32[]{:S(2)}) collective-permute-start(bf16[320,12,2]{0,2,1:T(2,128)(2,1)S(1)} %get-tuple-element.4), channel_id=1, source_target_pairs={{0,1},{1,2},{2,3},{4,5},{5,6},{6,7},{8,9},{9,10},{10,11},{12,13},{... | collective-permute-start | bytes 46088 | tf_op jit(solution)/shard_map/ppermute | solution.py:14
  24.0 0.8 %fusion.24 = f32[10,130,320]{2,1,0:T(8,128)S(1)} fusion(bf16[320,12,132]{0,2,1:T(8,128)(2,1)S(1)} %pad_maximum_fusion, bf16[9,320,320]{2,1,0:T(8,128)(2,1)S(1)} %copy-done.5), kind=kOutput, calls=%fused_computation.48 | convolution fusion | flops 266240000 | bytes 2954240 | tf_op jit(solution)/shard_map/oc,cwh->owh/dot_general | solution.py:28
  24.8 0.8 %fusion.26 = f32[10,130,320]{2,1,0:T(8,128)S(1)} fusion(bf16[320,12,132]{0,2,1:T(8,128)(2,1)S(1)} %pad_maximum_fusion, bf16[9,320,320]{2,1,0:T(8,128)(2,1)S(1)} %copy-done.5), kind=kOutput, calls=%fused_computation.50 | convolution fusion | flops 266240000 | bytes 2954240 | tf_op jit(solution)/shard_map/oc,cwh->owh/dot_general | solution.py:28
  25.6 0.8 %fusion.28 = f32[10,130,320]{2,1,0:T(8,128)S(1)} fusion(bf16[320,12,132]{0,2,1:T(8,128)(2,1)S(1)} %pad_maximum_fusion, bf16[9,320,320]{2,1,0:T(8,128)(2,1)S(1)} %copy-done.5), kind=kOutput, calls=%fused_computation.52 | convolution fusion | flops 266240000 | bytes 2954240 | tf_op jit(solution)/shard_map/oc,cwh->owh/dot_general | solution.py:28
  26.4 0.8 %fusion.79 = f32[10,130,320]{2,1,0:T(8,128)S(1)} fusion(bf16[9,320,320]{2,1,0:T(8,128)(2,1)S(1)} %copy-done.5, bf16[320,2,128]{0,2,1:T(8,128)(2,1)S(1)} %collective-permute-done.1, bf16[320,8,128]{0,2,1:T(8,128)(2,1)S(1)} %copy.12, bf16[320,2,128]{0,2,1:T(8,128)(2,1)S(1)} %collective-permute-done, bf16[320,12,2]{0,2,1:T(2,128)(2,1)S(1)} %collective-permute-done.2), kind=kOutput, calls=%fused_computation.104 | convolution fusion | flops 270233600 | bytes 3107840 | tf_op jit(solution)/shard_map/oc,cwh->owh/dot_general | solution.py:28
  27.2 0.8 %fusion.81 = f32[10,130,320]{2,1,0:T(8,128)S(1)} fusion(bf16[9,320,320]{2,1,0:T(8,128)(2,1)S(1)} %copy-done.5, bf16[320,12,2]{0,2,1:T(2,128)(2,1)S(1)} %collective-permute-done.3, bf16[320,2,128]{0,2,1:T(8,128)(2,1)S(1)} %collective-permute-done.1, bf16[320,8,128]{0,2,1:T(8,128)(2,1)S(1)} %copy.12, bf16[320,2,128]{0,2,1:T(8,128)(2,1)S(1)} %collective-permute-done), kind=kOutput, calls=%fused_computation.106 | convolution fusion | flops 270233600 | bytes 3107840 | tf_op jit(solution)/shard_map/oc,cwh->owh/dot_general | solution.py:28
  28.0 0.8 %fusion.84 = f32[10,130,320]{2,1,0:T(8,128)S(1)} fusion(bf16[9,320,320]{2,1,0:T(8,128)(2,1)S(1)} %copy-done.5, bf16[320,2,128]{0,2,1:T(8,128)(2,1)S(1)} %collective-permute-done.1, bf16[320,8,128]{0,2,1:T(8,128)(2,1)S(1)} %copy.12, bf16[320,2,128]{0,2,1:T(8,128)(2,1)S(1)} %collective-permute-done, bf16[320,12,2]{0,2,1:T(2,128)(2,1)S(1)} %collective-permute-done.2), kind=kOutput, calls=%fused_computation.109 | convolution fusion | flops 270233600 | bytes 3107840 | tf_op jit(solution)/shard_map/oc,cwh->owh/dot_general | solution.py:28
  28.8 0.8 %fusion.86 = f32[10,130,320]{2,1,0:T(8,128)S(1)} fusion(bf16[9,320,320]{2,1,0:T(8,128)(2,1)S(1)} %copy-done.5, bf16[320,12,2]{0,2,1:T(2,128)(2,1)S(1)} %collective-permute-done.3, bf16[320,2,128]{0,2,1:T(8,128)(2,1)S(1)} %collective-permute-done.1, bf16[320,8,128]{0,2,1:T(8,128)(2,1)S(1)} %copy.12, bf16[320,2,128]{0,2,1:T(8,128)(2,1)S(1)} %collective-permute-done), kind=kOutput, calls=%fused_computation.111 | convolution fusion | flops 270233600 | bytes 3107840 | tf_op jit(solution)/shard_map/oc,cwh->owh/dot_general | solution.py:28
  29.7 0.8 %fusion.89 = f32[10,130,320]{2,1,0:T(8,128)S(1)} fusion(bf16[9,320,320]{2,1,0:T(8,128)(2,1)S(1)} %copy-done.5, bf16[320,2,128]{0,2,1:T(8,128)(2,1)S(1)} %collective-permute-done.1, bf16[320,8,128]{0,2,1:T(8,128)(2,1)S(1)} %copy.12, bf16[320,2,128]{0,2,1:T(8,128)(2,1)S(1)} %collective-permute-done, bf16[320,12,2]{0,2,1:T(2,128)(2,1)S(1)} %collective-permute-done.2), kind=kOutput, calls=%fused_computation.114 | convolution fusion | flops 270233600 | bytes 3107840 | tf_op jit(solution)/shard_map/oc,cwh->owh/dot_general | solution.py:28
  30.5 2.3 %fusion.5 = bf16[320,10,130]{0,2,1:T(8,128)(2,1)S(1)} fusion(f32[10,130,320]{2,1,0:T(8,128)S(1)} %fusion.24, f32[10,130,320]{2,1,0:T(8,128)S(1)} %fusion.79, f32[10,130,320]{2,1,0:T(8,128)S(1)} %fusion.81, f32[10,130,320]{2,1,0:T(8,128)S(1)} %fusion.26, f32[10,130,320]{2,1,0:T(8,128)S(1)} %fusion.84, f32[10,130,320]{2,1,0:T(8,128)S(1)} %fusion.86, ...), kind=kOutput, calls=%fused_computation.9 | convolution fusion | flops 276473600 | bytes 18993664 | tf_op jit(solution)/shard_map/oc,cwh->owh/dot_general | solution.py:28
  38.0 1.7 %fusion.122 = (bf16[320,8,128]{2,0,1:T(8,128)(2,1)}, f32[320,8,128]{2,0,1:T(8,128)S(1)}) fusion(f32[320,8,128]{2,1,0:T(8,128)S(1)} %copy-done.3, f32[320]{0:T(512)S(1)} %copy-done.8, f32[8,128,320]{1,2,0:T(8,128)S(1)} %convolution_add_fusion.2, bf16[9,320,320]{2,1,0:T(8,128)(2,1)S(1)} %copy-done.2, bf16[320,10,130]{0,2,1:T(8,128)(2,1)S(1)} %fusion.5), kind=kOutput, calls=%fused_computation.157 | convolution fusion | flops 212336640 | bytes 5621760 | tf_op jit(solution)/shard_map/oc,cwh->owh/dot_general | solution.py:28
  39.8 5.2 %all-to-all-start = ((bf16[320,8,128]{2,0,1:T(8,128)(2,1)}), bf16[320,8,128]{2,0,1:T(8,128)(2,1)}, u32[]{:S(2)}, u32[]{:S(2)}) async-start(bf16[320,8,128]{2,0,1:T(8,128)(2,1)} %get-tuple-element.14), calls=%async_computation | async-start | bytes 1310720 | tf_op jit(solution)/shard_map/all_to_all | solution.py:67
  45.0 2.1 %fusion.10 = bf16[320,4,514]{2,0,1:T(8,128)(2,1)S(1)} fusion(bf16[320,1,512]{2,0,1:T(8,128)(2,1)} %collective-permute-done.5, bf16[320,2,512]{2,0,1:T(8,128)(2,1)S(1)} %copy.45, bf16[320,1,512]{2,0,1:T(8,128)(2,1)} %collective-permute-done.4), kind=kLoop, calls=%fused_computation.14 | loop fusion | flops 7895040 | bytes 2626560 | tf_op jit(solution)/shard_map/concatenate | solution.py:16
  50.0 1.5 %convolution_bitcast_fusion.3 = f32[320,2,512]{2,0,1:T(8,128)S(1)} fusion(bf16[320,1,512]{2,0,1:T(8,128)(2,1)} %collective-permute-done.5, bf16[320,2,512]{2,0,1:T(8,128)(2,1)S(1)} %copy.45, bf16[9,320,320]{2,1,0:T(8,128)(2,1)S(1)} %copy-done.1), kind=kOutput, calls=%fused_computation.38 | convolution fusion | flops 211025920 | bytes 2539520 | tf_op jit(solution)/shard_map/oc,cwh->owh/dot_general | solution.py:28
  51.5 1.5 %fusion.50 = f32[2,512,320]{1,2,0:T(8,128)S(1)} fusion(bf16[320,2,512]{2,0,1:T(8,128)(2,1)S(1)} %copy.45, bf16[320,1,512]{2,0,1:T(8,128)(2,1)} %collective-permute-done.4, bf16[9,320,320]{2,1,0:T(8,128)(2,1)S(1)} %copy-done.1), kind=kOutput, calls=%fused_computation.76 | convolution fusion | flops 211025920 | bytes 2539520 | tf_op jit(solution)/shard_map/oc,cwh->owh/dot_general | solution.py:28
  53.0 1.9 %fusion.23 = f32[320,2,512]{2,0,1:T(8,128)} fusion(f32[320,2,512]{2,0,1:T(8,128)S(1)} %convolution_bitcast_fusion.2, f32[320,2,512]{2,0,1:T(8,128)S(1)} %convolution_bitcast_fusion.3, f32[320,2,512]{2,0,1:T(8,128)S(1)} %convolution_bitcast_fusion.4, f32[320,2,512]{2,0,1:T(8,128)S(1)} %convolution_bitcast_fusion.5, f32[320,2,512]{2,0,1:T(8,128)S(1)} %fusion.59, ...), kind=kOutput, calls=%fused_computation.42 | convolution fusion | flops 212664320 | bytes 12699648 | tf_op jit(solution)/shard_map/oc,cwh->owh/dot_general | solution.py:28
  55.3 2.6 %fusion.123 = (bf16[320,2,512]{2,0,1:T(8,128)(2,1)S(1)}, f32[320,2,512]{2,0,1:T(8,128)S(1)}) fusion(bf16[4,2,40,8,128]{4,3,2,1,0:T(8,128)(2,1)} %bitcast.75, bf16[320,320]{1,0:T(8,128)(2,1)S(1)} %copy-done, f32[320,2,512]{2,1,0:T(2,128)} %param.11, f32[320,2,512]{2,0,1:T(8,128)} %fusion.23), kind=kOutput, calls=%fused_computation.158 | convolution fusion | flops 212008960 | bytes 5447680 | tf_op jit(solution)/shard_map/oc,cwh->owh/dot_general | solution.py:35
  58.0 0.9 %pad_maximum_fusion.6 = bf16[4,320,2,128]{3,1,2,0:T(8,128)(2,1)} fusion(bf16[1,320,2,128]{3,1,2,0:T(8,128)(2,1)S(1)} %get-tuple-element.9, bf16[1,320,2,128]{3,1,2,0:T(8,128)(2,1)S(1)} %get-tuple-element.10, bf16[1,320,2,128]{3,1,2,0:T(8,128)(2,1)S(1)} %get-tuple-element.11, bf16[1,320,2,128]{3,1,2,0:T(8,128)(2,1)S(1)} %get-tuple-element.8), kind=kLoop, calls=%fused_computation.79 | loop fusion | flops 983040 | bytes 1310720 | tf_op jit(solution)/shard_map/stack | solution.py:71
  59.0 4.0 %all-to-all-start.1 = ((bf16[4,320,2,128]{3,1,2,0:T(8,128)(2,1)}), bf16[4,320,2,128]{3,1,2,0:T(8,128)(2,1)S(1)}, u32[]{:S(2)}, u32[]{:S(2)}) async-start(bf16[4,320,2,128]{3,1,2,0:T(8,128)(2,1)} %pad_maximum_fusion.6), calls=%async_computation.1 | async-start | bytes 1310720 | tf_op jit(solution)/shard_map/all_to_all | solution.py:72
  63.0 2.1 %copy.27 = f32[320,2,512]{2,1,0:T(2,128)} copy(f32[320,2,512]{2,0,1:T(8,128)S(1)} %get-tuple-element.17) | data formatting | bytes 2621440
  65.0 8.2 %all-to-all-done.1 = bf16[4,320,2,128]{3,1,2,0:T(8,128)(2,1)S(1)} async-done(((bf16[4,320,2,128]{3,1,2,0:T(8,128)(2,1)}), bf16[4,320,2,128]{3,1,2,0:T(8,128)(2,1)S(1)}, u32[]{:S(2)}, u32[]{:S(2)}) %all-to-all-start.1) | async-done | bytes 655392 | tf_op jit(solution)/shard_map/all_to_all | solution.py:72
  73.2 1.4 %fusion.20 = f32[320,8,128]{2,0,1:T(8,128)S(1)} fusion(f32[320,8,128]{2,0,1:T(8,128)S(1)} %get-tuple-element.15, bf16[320,8,128]{2,0,1:T(8,128)(2,1)S(1)} %bitcast.191, bf16[320,320]{1,0:T(8,128)(2,1)} %param.19), kind=kOutput, calls=%fused_computation.34 | convolution fusion | flops 210042880 | bytes 3481600 | tf_op jit(solution)/shard_map/oc,cwh->owh/dot_general | solution.py:35
  74.6 1.8 %copy.26 = f32[320,8,128]{2,1,0:T(8,128)} copy(f32[320,8,128]{2,0,1:T(8,128)S(1)} %fusion.20) | data formatting | bytes 2621440
  (45 shorter events, 10.0 us)
Async XLA Ops:
  0.6 54.7 %copy-start = (bf16[320,320]{1,0:T(8,128)(2,1)S(1)}, bf16[320,320]{1,0:T(8,128)(2,1)}, u32[]{:S(2)}) copy-start(bf16[320,320]{1,0:T(8,128)(2,1)} %param.18) | copy-start | bytes 614404
  0.6 9.5 %copy-start.4 = (f32[320,2,512]{2,1,0:T(2,128)S(1)}, f32[320,2,512]{2,1,0:T(2,128)}, u32[]{:S(2)}) copy-start(f32[320,2,512]{2,1,0:T(2,128)} %param.11) | copy-start | bytes 3932164
  3.3 14.5 %collective-permute-start.1 = (bf16[320,2,128]{0,2,1:T(8,128)(2,1)}, bf16[320,2,128]{0,2,1:T(8,128)(2,1)S(1)}, u32[]{:S(2)}, u32[]{:S(2)}) collective-permute-start(bf16[320,2,128]{0,2,1:T(8,128)(2,1)} %get-tuple-element.7), channel_id=1, source_target_pairs={{4,0},{8,4},{12,8},{5,1},{9,5},{13,9},{6,2},{10,6},{14,10},{7,3},{... | collective-permute-start | bytes 491528 | tf_op jit(solution)/shard_map/ppermute | solution.py:15
  4.5 13.2 %collective-permute-start = (bf16[320,2,128]{0,2,1:T(8,128)(2,1)}, bf16[320,2,128]{0,2,1:T(8,128)(2,1)S(1)}, u32[]{:S(2)}, u32[]{:S(2)}) collective-permute-start(bf16[320,2,128]{0,2,1:T(8,128)(2,1)} %get-tuple-element.6), channel_id=1, source_target_pairs={{0,4},{4,8},{8,12},{1,5},{5,9},{9,13},{2,6},{6,10},{10,14},{3,7},{... | collective-permute-start | bytes 491528 | tf_op jit(solution)/shard_map/ppermute | solution.py:14
  11.2 33.7 %collective-permute-start.5 = (bf16[320,1,512]{2,0,1:T(8,128)(2,1)}, bf16[320,1,512]{2,0,1:T(8,128)(2,1)}, u32[]{:S(2)}, u32[]{:S(2)}) collective-permute-start(bf16[320,1,512]{2,0,1:T(8,128)(2,1)} %get-tuple-element.13), channel_id=1, source_target_pairs={{1,0},{2,1},{3,2},{4,3},{5,4},{6,5},{7,6},{8,7},{9,8},{10,9},{11,1... | collective-permute-start | bytes 983048 | tf_op jit(solution)/shard_map/ppermute | solution.py:15
  12.5 32.5 %collective-permute-start.4 = (bf16[320,1,512]{2,0,1:T(8,128)(2,1)}, bf16[320,1,512]{2,0,1:T(8,128)(2,1)}, u32[]{:S(2)}, u32[]{:S(2)}) collective-permute-start(bf16[320,1,512]{2,0,1:T(8,128)(2,1)} %get-tuple-element.12), channel_id=1, source_target_pairs={{0,1},{1,2},{2,3},{3,4},{4,5},{5,6},{6,7},{7,8},{8,9},{9,10},{10,1... | collective-permute-start | bytes 983048 | tf_op jit(solution)/shard_map/ppermute | solution.py:14
  17.8 6.2 %copy-start.5 = (bf16[9,320,320]{2,1,0:T(8,128)(2,1)S(1)}, bf16[9,320,320]{2,1,0:T(8,128)(2,1)}, u32[]{:S(2)}) copy-start(bf16[9,320,320]{2,1,0:T(8,128)(2,1)} %param.12) | copy-start | bytes 5529604
  17.8 4.9 %collective-permute-start.3 = (bf16[320,12,2]{0,2,1:T(2,128)(2,1)S(1)}, bf16[320,12,2]{0,2,1:T(2,128)(2,1)S(1)}, u32[]{:S(2)}, u32[]{:S(2)}) collective-permute-start(bf16[320,12,2]{0,2,1:T(2,128)(2,1)S(1)} %get-tuple-element.5), channel_id=1, source_target_pairs={{1,0},{2,1},{3,2},{5,4},{6,5},{7,6},{9,8},{10,9},{11,10},{13,12},{... | collective-permute-start | bytes 46088 | tf_op jit(solution)/shard_map/ppermute | solution.py:15
  19.3 4.2 %collective-permute-start.2 = (bf16[320,12,2]{0,2,1:T(2,128)(2,1)S(1)}, bf16[320,12,2]{0,2,1:T(2,128)(2,1)S(1)}, u32[]{:S(2)}, u32[]{:S(2)}) collective-permute-start(bf16[320,12,2]{0,2,1:T(2,128)(2,1)S(1)} %get-tuple-element.4), channel_id=1, source_target_pairs={{0,1},{1,2},{2,3},{4,5},{5,6},{6,7},{8,9},{9,10},{10,11},{12,13},{... | collective-permute-start | bytes 46088 | tf_op jit(solution)/shard_map/ppermute | solution.py:14
  29.6 0.8 %copy-start.7 = (f32[320]{0:T(512)S(1)}, f32[320]{0:T(512)}, u32[]{:S(2)}) copy-start(f32[320]{0:T(512)} %param.15) | copy-start | bytes 3844
  30.5 2.4 %copy-start.2 = (bf16[9,320,320]{2,1,0:T(8,128)(2,1)S(1)}, bf16[9,320,320]{2,1,0:T(8,128)(2,1)}, u32[]{:S(2)}) copy-start(bf16[9,320,320]{2,1,0:T(8,128)(2,1)} %param.13) | copy-start | bytes 5529604
  36.7 1.3 %copy-start.3 = (f32[320,8,128]{2,1,0:T(8,128)S(1)}, f32[320,8,128]{2,1,0:T(8,128)}, u32[]{:S(2)}) copy-start(f32[320,8,128]{2,1,0:T(8,128)} %param.10) | copy-start | bytes 3932164
  36.7 1.3 %copy-start.8 = (f32[320]{0:T(512)S(1)}, f32[320]{0:T(512)}, u32[]{:S(2)}) copy-start(f32[320]{0:T(512)} %param.16) | copy-start | bytes 3844
  39.8 15.5 %all-to-all-start = ((bf16[320,8,128]{2,0,1:T(8,128)(2,1)}), bf16[320,8,128]{2,0,1:T(8,128)(2,1)}, u32[]{:S(2)}, u32[]{:S(2)}) async-start(bf16[320,8,128]{2,0,1:T(8,128)(2,1)} %get-tuple-element.14), calls=%async_computation | async-start | bytes 1310720 | tf_op jit(solution)/shard_map/all_to_all | solution.py:67
  45.0 2.1 %copy-start.1 = (bf16[9,320,320]{2,1,0:T(8,128)(2,1)S(1)}, bf16[9,320,320]{2,1,0:T(8,128)(2,1)}, u32[]{:S(2)}) copy-start(bf16[9,320,320]{2,1,0:T(8,128)(2,1)} %param.14) | copy-start | bytes 5529604
  51.5 1.5 %copy-start.6 = (f32[320]{0:T(512)S(1)}, f32[320]{0:T(512)}, u32[]{:S(2)}) copy-start(f32[320]{0:T(512)} %param.17) | copy-start | bytes 3844
  59.0 14.2 %all-to-all-start.1 = ((bf16[4,320,2,128]{3,1,2,0:T(8,128)(2,1)}), bf16[4,320,2,128]{3,1,2,0:T(8,128)(2,1)S(1)}, u32[]{:S(2)}, u32[]{:S(2)}) async-start(bf16[4,320,2,128]{3,1,2,0:T(8,128)(2,1)} %pad_maximum_fusion.6), calls=%async_computation.1 | async-start | bytes 1310720 | tf_op jit(solution)/shard_map/all_to_all | solution.py:72
